TPU v7x, 32 devices: a whole 2x2x4 slice. The times are simulated.
32 devices in a mesh: dp: 4 (over z), fsdp: 4 (over x, core), tensor: 2 (over y).
Axes of the slice: x: 2, y: 2, z: 4, core: 2. Of those that a mesh axis runs over, the one named last changes fastest.
Arguments:
- tokens: bfloat16 [4096, 8192], P(('dp', 'fsdp'), 'tensor'), may hold values from -700 to 700
- queries: bfloat16 [4096, 8192], P(('dp', 'fsdp'), 'tensor'), may hold values from -140 to 140
- segment_ids: int32 [32, 128], P(('dp', 'fsdp')), may hold values from 0 to 3, never falling along the last dimension, each value on 1 to 64 neighbouring positions
- gain: float32 [8192], P('tensor'), may hold values from 0.1 to 1.9
- key_value_weight: bfloat16 [8192, 2048], P('tensor', 'fsdp'), may hold values from -0.0625 to 0.0625
- plan: int32 [8], replicated, may hold values from 0 to 7, as said below
Outputs:
- attended: bfloat16 [4096, 8192], P(('dp', 'fsdp'), 'tensor')
Inputs may be any that keep to these rules, and one draw needn't show every extreme that they name: plan is a permutation of 0 to 7; from one dp index to another at most 1 micro-batches go, and in every draw some pair of dp indices carries exactly 1.
All inputs are finite; a program needn't handle non-finite values.
Results may differ from a plain program's by a relative error of at most 0.011.
Values may be sent and summed in bfloat16 or wider, within the bound.
A program may use at most 64 MiB of HBM per device.

v0:
```python
import jax
import jax.numpy as jnp
from jax import lax
from jax.sharding import PartitionSpec as P

HEAD_SIZE = 128


epsilon = 1e-05


def pack_rows(send_index, send_valid, flat_rows, length):
    ranks_here = send_index.shape[0]
    slots_here = send_index.shape[1]
    taken = jnp.take(flat_rows, send_index.reshape(-1), axis=0)
    sent = taken * send_valid.astype(flat_rows.dtype)
    return sent.reshape(ranks_here, slots_here, length, -1)


def unpack_rows(keep_index, arrived):
    flat = arrived.reshape(arrived.shape[0] * arrived.shape[1], -1)
    return jnp.take(flat, keep_index, axis=0)


def project(rows, gain, key_value_weight):
    values = rows.astype(jnp.float32)
    stats = lax.psum(jnp.sum(values * values, axis=1), "tensor")
    full_width = rows.shape[1] * lax.axis_size("tensor")
    scale = lax.rsqrt(stats / full_width + epsilon)
    normed = (values * scale[:, None] * gain).astype(jnp.bfloat16)
    partial_value = jnp.dot(
        normed,
        lax.all_gather(key_value_weight, "fsdp", axis=1, tiled=True),
        preferred_element_type=jnp.float32,
    )
    return lax.psum_scatter(partial_value, "tensor", scatter_dimension=1, tiled=True)


def attend(query_row_block, key_value_rows, documents):
    batches, length = documents.shape
    heads_kv = key_value_rows.shape[1] // (2 * HEAD_SIZE)
    head_group = query_row_block.shape[1] // (heads_kv * HEAD_SIZE)
    query_head_count = query_row_block.astype(jnp.float32).reshape(
        batches, length, heads_kv, head_group, HEAD_SIZE
    )
    key_value_heads = key_value_rows.reshape(batches, length, heads_kv, 2, HEAD_SIZE)
    scores = jnp.einsum(
        "mqhgd,mkhd->mhgqk",
        query_head_count,
        key_value_heads[:, :, :, 0],
        precision=lax.Precision.HIGHEST,
    ) * HEAD_SIZE ** (-0.5)
    positions = jnp.arange(length, dtype=jnp.int32)
    causal = positions[:, None] >= positions[None, :]
    allowed = (documents[:, :, None] == documents[:, None, :]) & causal[None]
    scores = jnp.where(allowed[:, None, None], scores, -1e30)
    row_max = jnp.max(scores, axis=-1, keepdims=True)
    expo = jnp.exp(scores - row_max)
    weights = (expo / jnp.sum(expo, axis=-1, keepdims=True)).astype(jnp.bfloat16)
    mixed = jnp.einsum(
        "mhgqk,mkhd->mqhgd",
        weights.astype(jnp.float32),
        key_value_heads[:, :, :, 1],
        precision=lax.Precision.HIGHEST,
    )
    return mixed.reshape(batches * length, -1).astype(jnp.bfloat16)


def shards(tokens, queries, segment_ids, gain, key_value_weight, plan):
    rank_count = lax.axis_size("dp")
    own_rank = lax.axis_index("dp")
    batches = segment_ids.shape[0]
    length = segment_ids.shape[1]
    slot_cap = (batches + rank_count - 1) // rank_count
    dest_rank = plan.reshape(rank_count, batches) // batches
    slot_range = jnp.arange(batches, dtype=jnp.int32)
    same_dest = dest_rank[:, :, None] == dest_rank[:, None, :]
    earlier = slot_range[None, None, :] < slot_range[None, :, None]
    arrival = jnp.sum((same_dest & earlier).astype(jnp.int32), axis=2)
    own_dest = lax.dynamic_index_in_dim(dest_rank, own_rank, 0, keepdims=False)
    own_arrival = lax.dynamic_index_in_dim(arrival, own_rank, 0, keepdims=False)
    rank_range = jnp.arange(rank_count, dtype=jnp.int32)
    cap_range = jnp.arange(slot_cap, dtype=jnp.int32)
    send_hits = (
        (own_dest[None, None, :] == rank_range[:, None, None])
        & (own_arrival[None, None, :] == cap_range[None, :, None])
    ).astype(jnp.int32)
    send_index = jnp.sum(send_hits * slot_range[None, None, :], axis=2)
    send_valid = jnp.sum(send_hits, axis=2)
    inverse = jnp.argsort(plan)
    sources = lax.dynamic_slice_in_dim(inverse, own_rank * batches, batches)
    source_rank = sources // batches
    source_arrival = jnp.take(arrival.reshape(-1), sources)
    keep_index = source_rank * slot_cap + source_arrival
    local_kv = project(tokens, gain, key_value_weight)
    results = attend(queries, local_kv, segment_ids)
    parcel = pack_rows(send_index, send_valid, results.reshape(batches, -1), length)
    arrived = lax.all_to_all(parcel, "dp", split_axis=0, concat_axis=0, tiled=True)
    return unpack_rows(keep_index, arrived).reshape(batches * length, -1)


def solution(mesh):
    placed = (
        P(("dp", "fsdp"), "tensor"),
        P(("dp", "fsdp"), "tensor"),
        P(("dp", "fsdp"), None),
        P("tensor"),
        P("tensor", "fsdp"),
        P(),
    )
    return jax.shard_map(
        shards, mesh=mesh, in_specs=placed, out_specs=P(("dp", "fsdp"), "tensor"), check_vma=False
    )
```

profile of v0, /device:TPU:0, one launch (start us, length us, event | category | flops | bytes accessed | tf_op | source)
XLA Modules:
  0.0 353.8 jit_solution(198439708201820833)
XLA Ops:
  6.5 0.7 all-gather.2.cloned.1.call-update
  7.3 0.8 copy-done.1
  8.1 0.5 fusion.1
  8.6 5.9 %psum.7 = f32[256]{0:T(256)S(1)} all-reduce(f32[256]{0:T(256)S(1)} %fusion.1), channel_id=1, replica_groups=mesh['dp'=4,'fsdp'=4,'tensor'=2] {'tensor'}, use_global_device_ids=true, to_apply=%region_4.5 | all-reduce | flops 256 | bytes 2048 | tf_op jit(solution)/shard_map/psum | solution.py:27
  14.5 103.0 %all-gather.2.cloned.1.call-done = bf16[4096,2048]{1,0:T(8,128)(2,1)} async-done(((bf16[4096,512]{1,0:T(8,128)(2,1)}), bf16[4096,2048]{1,0:T(8,128)(2,1)}) %all-gather.2.cloned.1.call-update) | async-done | bytes 16777232 | tf_op jit(solution)/shard_map/all_gather | solution.py:33
  117.6 9.5 %fusion.7 = f32[256,2048]{1,0:T(8,128)} fusion(bf16[4096,2048]{1,0:T(8,128)(2,1)} %all-gather.2.cloned.1.call-done, bf16[256,4096]{1,0:T(8,128)(2,1)S(1)} %copy-done.1, f32[4096]{0:T(1024)S(1)} %copy-done.6, f32[256]{0:T(256)S(1)} %add_rsqrt_fusion), kind=kOutput, calls=%fused_computation.24 | convolution fusion | flops 4299161600 | bytes 20988928 | tf_op jit(solution)/shard_map/dot_general | solution.py:31
  127.2 1.0 sort.17
  128.9 2.1 copy.36
  131.1 0.6 gather_fusion
  132.0 27.2 %reduce-scatter.2.cloned.1.call-done = f32[256,1024]{1,0:T(8,128)} async-done(((f32[256,2048]{1,0:T(8,128)}), f32[256,1024]{1,0:T(8,128)}) %reduce-scatter.2.cloned.1.call-update) | async-done | bytes 1048592 | tf_op jit(solution)/shard_map/reduce_scatter | solution.py:36
  159.1 2.1 reshape.309
  161.3 1.8 fusion.27
  163.0 1.2 copy.34
  164.3 3.1 fusion.9
  167.4 1.1 fusion.28
  168.5 3.1 convert_bitcast_fusion
  171.6 3.4 copy.29
  175.1 18.0 %copy.46 = bf16[1,2,4096,128]{3,1,2,0:T(2,128)(2,1)S(1)} copy(bf16[1,2,4096,128]{3,2,1,0:T(8,128)(2,1)S(1)} %bitcast.65) | data formatting | bytes 4194304
  193.1 0.3 mini-gather-slice.14
  193.4 1.2 fusion.26
  194.5 2.2 gather_fusion.5
  196.7 1.4 gather_fusion.4
  198.1 1.4 gather_fusion.3
  199.5 1.4 gather_fusion.2
  200.9 2.2 gather_fusion.1
  203.1 1.5 constant_dynamic-update-slice_fusion.4
  204.6 0.3 constant_dynamic-update-slice_fusion.3
  204.9 0.4 constant_dynamic-update-slice_fusion.2
  205.3 0.3 constant_dynamic-update-slice_fusion.1
  205.7 0.4 constant_dynamic-update-slice_fusion
  206.0 6.8 %fusion.5 = bf16[4,1,128,4096]{3,2,1,0:T(8,128)(2,1)} fusion(bf16[1,4,128,4096]{3,1,2,0:T(4,128)(2,1)S(1)} %bitcast.66, pred[4]{0:T(512)(128)(4,1)S(1)} %compare_and_fusion.1, bf16[4]{0:T(256)(128)(2,1)S(1)} %convert_element_type.51), kind=kLoop, calls=%fused_computation.19 | loop fusion | flops 4194304 | bytes 8388620 | tf_op jit(solution)/shard_map/mul | solution.py:16
  212.9 5.1 %all-to-all-start = ((bf16[4,1,128,4096]{3,2,1,0:T(8,128)(2,1)}), bf16[4,1,128,4096]{3,2,1,0:T(8,128)(2,1)}, u32[]{:S(2)}, u32[]{:S(2)}) async-start(bf16[4,1,128,4096]{3,2,1,0:T(8,128)(2,1)} %fusion.5), calls=%async_computation.1 | async-start | bytes 8388608 | tf_op jit(solution)/shard_map/all_to_all | solution.py:98
  218.0 93.0 %all-to-all-done = bf16[4,1,128,4096]{3,2,1,0:T(8,128)(2,1)} async-done(((bf16[4,1,128,4096]{3,2,1,0:T(8,128)(2,1)}), bf16[4,1,128,4096]{3,2,1,0:T(8,128)(2,1)}, u32[]{:S(2)}, u32[]{:S(2)}) %all-to-all-start) | async-done | bytes 4194336 | tf_op jit(solution)/shard_map/all_to_all | solution.py:98
  311.1 5.4 %copy.39 = bf16[1,4,128,4096]{3,1,2,0:T(4,128)(2,1)S(1)} copy(bf16[1,4,128,4096]{3,2,1,0:T(8,128)(2,1)} %bitcast.26) | data formatting | bytes 8388608
  316.5 1.2 mini-gather-slice.19
  317.7 1.2 fusion.25
  318.8 12.5 %gather_fusion.10 = bf16[2,104448]{1,0:T(2,128)(2,1)} fusion(bf16[4,104448]{1,0:T(4,128)(2,1)} %mini-gather-slice.19, s32[1024]{0:T(1024)S(1)} %get-tuple-element.23), kind=kCustom, calls=%fused_computation.10 | custom fusion | bytes 835592 | tf_op jit(solution)/shard_map/jit(_take)/gather | solution.py:22
  331.4 1.8 gather_fusion.9
  333.2 1.1 gather_fusion.8
  334.3 1.1 gather_fusion.7
  335.5 1.1 gather_fusion.6
  336.6 1.0 constant_dynamic-update-slice_fusion.9
  337.6 1.0 constant_dynamic-update-slice_fusion.8
  338.7 1.0 constant_dynamic-update-slice_fusion.7
  339.7 1.0 constant_dynamic-update-slice_fusion.6
  340.7 1.0 constant_dynamic-update-slice_fusion.5
  341.8 3.6 %gather.20 = bf16[256,4096]{1,0:T(8,128)(2,1)S(1)} reshape(bf16[2,524288]{1,0:T(2,128)(2,1)} %constant_dynamic-update-slice_fusion.5) | data formatting | bytes 4194304 | tf_op jit(solution)/shard_map/jit(_take)/gather | solution.py:22
  345.4 1.6 broadcast_select_fusion
  (38 shorter events, 1.2 us)
Async XLA Ops:
  6.5 1.6 copy-start.1
  6.5 111.0 %copy-start.6 = (f32[4096]{0:T(1024)S(1)}, f32[4096]{0:T(1024)}, u32[]{:S(2)}) copy-start(f32[4096]{0:T(1024)} %param.9) | copy-start | bytes 49156
  6.5 111.0 %all-gather.2.cloned.1.call-start = ((), (), s32[]{:S(2)}) async-start(), calls=%async_computation.2 | async-start | bytes 20971520 | tf_op jit(solution)/shard_map/all_gather | solution.py:33
  7.3 151.9 %reduce-scatter.2.cloned.1.call-start = ((), (), s32[]{:S(2)}) async-start(), calls=%async_computation.3 | async-start | bytes 3145728 | tf_op jit(solution)/shard_map/reduce_scatter | solution.py:36
  14.5 112.6 %copy-start.5 = (s32[8]{0:T(128)S(1)}, s32[8]{0:T(128)}, u32[]{:S(2)}) copy-start(s32[8]{0:T(128)} %param.11) | copy-start | bytes 100
  127.1 4.8 %copy-start.4 = (s32[2,128]{1,0:T(2,128)S(1)}, s32[2,128]{1,0:T(2,128)}, u32[]{:S(2)}) copy-start(s32[2,128]{1,0:T(2,128)} %param.8) | copy-start | bytes 3076
  203.1 2.6 copy-start
  212.9 98.2 %all-to-all-start = ((bf16[4,1,128,4096]{3,2,1,0:T(8,128)(2,1)}), bf16[4,1,128,4096]{3,2,1,0:T(8,128)(2,1)}, u32[]{:S(2)}, u32[]{:S(2)}) async-start(bf16[4,1,128,4096]{3,2,1,0:T(8,128)(2,1)} %fusion.5), calls=%async_computation.1 | async-start | bytes 8388608 | tf_op jit(solution)/shard_map/all_to_all | solution.py:98
  334.3 5.4 %copy-start.2 = (bf16[2,104960]{1,0:T(2,128)(2,1)S(1)}, bf16[2,104960]{1,0:T(2,128)(2,1)}, u32[]{:S(2)}) copy-start(bf16[2,104960]{1,0:T(2,128)(2,1)} %gather_fusion.9) | copy-start | bytes 1259524
  335.5 5.3 %copy-start.3 = (bf16[2,104448]{1,0:T(2,128)(2,1)S(1)}, bf16[2,104448]{1,0:T(2,128)(2,1)}, u32[]{:S(2)}) copy-start(bf16[2,104448]{1,0:T(2,128)(2,1)} %gather_fusion.10) | copy-start | bytes 1253380
Sparse Core Ops, SparseCore 0:
  8.9 108.6 all-gather.1
  127.2 31.8 reduce-scatter.1
where the time goes:
time: 355 us; the launch traced here: 354 us
  waiting for transfers between devices  224 us (63%)
  local copies, waits for them, and re-layouts  77.7 us (22%)
  matrix products  15.7 us (4%)
  between operations  13.6 us (4%)
  other arithmetic  11.8 us (3%)
  blocking collectives  5.89 us (2%)
  starting transfers between devices  5.12 us (1%)
    all_gather x1, waiting for transfers between devices, project(): lax.all_gather(key_value_weight, 'fsdp', axis=1, tiled=True)  103 us
    all_to_all x1, waiting for transfers between devices, shards(): lax.all_to_all(parcel, 'dp', split_axis=0, concat_axis=0, tiled=True)  93 us
    unnamed x28, local copies, waits for them, and re-layouts  35.7 us
    reduce_scatter x1, waiting for transfers between devices, project(): lax.psum_scatter(partial_value, 'tensor', scatter_dimension=1, tiled=True)  27.2 us
    gather x8, local copies, waits for them, and re-layouts, unpack_rows(): return jnp.take(flat, keep_index, axis=0)  23.6 us
    gather x7, local copies, waits for them, and re-layouts, pack_rows(): taken = jnp.take(flat_rows, send_index.reshape(-1), axis=0)  9.97 us
    dot_general x1, matrix products, project(): jnp.dot(normed, lax.all_gather(key_value_weight, 'fsdp', axis=1, tiled=Tr...  9.51 us
  transfers between devices with their start and end apart: 3, of which 3 were waited for; matrix products, arithmetic and copies ran while one was open for 2% of the time, Pallas kernels for 0%

commit v1 on v0

v1 whole, which is shorter than its diff:
```python
import functools

import jax
import jax.numpy as jnp
from jax import lax
from jax.experimental import pallas as pl
from jax.experimental.pallas import tpu as pltpu
from jax.sharding import PartitionSpec as P

HEAD_SIZE = 128


epsilon = 1e-05


def pack_query_kernel(send_ref, query_ref, out_ref):
    out_ref[...] = query_ref[...]


def pack_queries(send_index, queries, length):
    ranks = send_index.shape[0]
    width = queries.shape[1]
    return pl.pallas_call(
        pack_query_kernel,
        grid_spec=pltpu.PrefetchScalarGridSpec(
            num_scalar_prefetch=1,
            grid=(ranks,),
            in_specs=[pl.BlockSpec((length, width), lambda r, send: (send[r], 0))],
            out_specs=pl.BlockSpec((length, width), lambda r, send: (r, 0)),
        ),
        out_shape=jax.ShapeDtypeStruct((ranks * length, width), queries.dtype),
        name="pack_queries",
    )(send_index, queries)


def pack_kv_kernel(heads_kv, send_ref, kv_ref, document_ref, out_ref):
    for h in range(heads_kv):
        key = kv_ref[:, 2 * h * HEAD_SIZE : (2 * h + 1) * HEAD_SIZE]
        high = key.astype(jnp.bfloat16)
        low = (key - high.astype(jnp.float32)).astype(jnp.bfloat16)
        value = kv_ref[:, (2 * h + 1) * HEAD_SIZE : (2 * h + 2) * HEAD_SIZE]
        for place, part in enumerate((high, low, value.astype(jnp.bfloat16))):
            start = (place * heads_kv + h) * HEAD_SIZE
            out_ref[:, start : start + HEAD_SIZE] = part
    out_ref[:, 3 * heads_kv * HEAD_SIZE :] = document_ref[...]


def pack_kv(send_index, kv, documents, length):
    ranks = send_index.shape[0]
    width = kv.shape[1]
    heads_kv = width // (2 * HEAD_SIZE)
    packed = (3 * heads_kv + 1) * HEAD_SIZE
    return pl.pallas_call(
        functools.partial(pack_kv_kernel, heads_kv),
        grid_spec=pltpu.PrefetchScalarGridSpec(
            num_scalar_prefetch=1,
            grid=(ranks,),
            in_specs=[
                pl.BlockSpec((length, width), lambda r, send: (send[r], 0)),
                pl.BlockSpec((length, HEAD_SIZE), lambda r, send: (send[r], 0)),
            ],
            out_specs=pl.BlockSpec((length, packed), lambda r, send: (r, 0)),
        ),
        out_shape=jax.ShapeDtypeStruct((ranks * length, packed), jnp.bfloat16),
        name="pack_kv",
    )(send_index, kv, documents)


def attend_kernel(
    head_group, keep_ref, query_ref, high_ref, low_ref, value_ref, document_ref, out_ref
):
    length = query_ref.shape[0]
    query = jnp.concatenate(
        [query_ref[:, g * HEAD_SIZE : (g + 1) * HEAD_SIZE] for g in range(head_group)], axis=0
    )
    across = (((1,), (1,)), ((), ()))
    scores = lax.dot_general(query, high_ref[...], across, preferred_element_type=jnp.float32)
    scores += lax.dot_general(query, low_ref[...], across, preferred_element_type=jnp.float32)
    scores = (scores * HEAD_SIZE ** (-0.5)).reshape(head_group, length, length)
    document = document_ref[...].astype(jnp.float32)
    rows = lax.broadcasted_iota(jnp.int32, (length, length), 0)
    columns = lax.broadcasted_iota(jnp.int32, (length, length), 1)
    allowed = (document == document.T) & (columns <= rows)
    scores = jnp.where(allowed[None], scores, -1e30)
    row_max = jnp.max(scores, axis=-1, keepdims=True)
    expo = jnp.exp(scores - row_max)
    weights = (expo / jnp.sum(expo, axis=-1, keepdims=True)).astype(jnp.bfloat16)
    mixed = jnp.dot(
        weights.reshape(head_group * length, length),
        value_ref[...],
        preferred_element_type=jnp.float32,
    ).astype(jnp.bfloat16)
    for g in range(head_group):
        out_ref[:, g * HEAD_SIZE : (g + 1) * HEAD_SIZE] = mixed[g * length : (g + 1) * length]


def attend(keep_index, queries, packed, length):
    batches = keep_index.shape[0]
    heads_kv = (packed.shape[1] // HEAD_SIZE - 1) // 3
    width = queries.shape[1]
    group_width = width // heads_kv

    def part(place):
        return pl.BlockSpec(
            (length, HEAD_SIZE), lambda s, h, keep: (keep[s], place * heads_kv + h)
        )

    return pl.pallas_call(
        functools.partial(attend_kernel, group_width // HEAD_SIZE),
        grid_spec=pltpu.PrefetchScalarGridSpec(
            num_scalar_prefetch=1,
            grid=(batches, heads_kv),
            in_specs=[
                pl.BlockSpec((length, group_width), lambda s, h, keep: (keep[s], h)),
                part(0),
                part(1),
                part(2),
                pl.BlockSpec((length, HEAD_SIZE), lambda s, h, keep: (keep[s], 3 * heads_kv)),
            ],
            out_specs=pl.BlockSpec((length, group_width), lambda s, h, keep: (s, h)),
        ),
        out_shape=jax.ShapeDtypeStruct((batches * length, width), jnp.bfloat16),
        name="attend",
    )(keep_index, queries, packed, packed, packed, packed)


def project(rows, gain, key_value_weight):
    values = rows.astype(jnp.float32)
    stats = lax.psum(jnp.sum(values * values, axis=1), "tensor")
    full_width = rows.shape[1] * lax.axis_size("tensor")
    scale = lax.rsqrt(stats / full_width + epsilon)
    normed = (values * scale[:, None] * gain).astype(jnp.bfloat16)
    partial_value = jnp.dot(
        normed,
        lax.all_gather(key_value_weight, "fsdp", axis=1, tiled=True),
        preferred_element_type=jnp.float32,
    )
    return lax.psum_scatter(partial_value, "tensor", scatter_dimension=1, tiled=True)


def shards(tokens, queries, segment_ids, gain, key_value_weight, plan):
    rank_count = lax.axis_size("dp")
    own_rank = lax.axis_index("dp")
    batches, length = segment_ids.shape
    own_dest = lax.dynamic_slice_in_dim(plan, own_rank * batches, batches) // batches
    rank_range = jnp.arange(rank_count, dtype=jnp.int32)
    slot_range = jnp.arange(batches, dtype=jnp.int32)
    send_index = jnp.sum(
        jnp.where(own_dest[None, :] == rank_range[:, None], slot_range[None, :], 0), axis=1
    )
    position = jnp.arange(plan.shape[0], dtype=jnp.int32)
    own_slots = own_rank * batches + slot_range
    keep_index = jnp.sum(
        jnp.where(plan[None, :] == own_slots[:, None], position[None, :] // batches, 0), axis=1
    )
    moved_queries = lax.all_to_all(
        pack_queries(send_index, queries, length), "dp", split_axis=0, concat_axis=0, tiled=True
    )
    documents = jnp.broadcast_to(
        segment_ids.reshape(batches * length, 1).astype(jnp.bfloat16),
        (batches * length, HEAD_SIZE),
    )
    kv = project(tokens, gain, key_value_weight)
    moved_kv = lax.all_to_all(
        pack_kv(send_index, kv, documents, length), "dp", split_axis=0, concat_axis=0, tiled=True
    )
    return attend(keep_index, moved_queries, moved_kv, length)


def solution(mesh):
    placed = (
        P(("dp", "fsdp"), "tensor"),
        P(("dp", "fsdp"), "tensor"),
        P(("dp", "fsdp"), None),
        P("tensor"),
        P("tensor", "fsdp"),
        P(),
    )
    return jax.shard_map(
        shards, mesh=mesh, in_specs=placed, out_specs=P(("dp", "fsdp"), "tensor"), check_vma=False
    )
```

time: 355 us -> 226 us (0.64)
  local copies, waits for them, and re-layouts: 77.7 us -> 1.94 us
  waiting for transfers between devices: 224 us -> 164 us
  Pallas kernels: 0 us -> 19.4 us
  other arithmetic: 11.8 us -> 1.94 us
  matrix products: 15.7 us -> 9.54 us
  starting transfers between devices: 5.12 us -> 9.21 us
    all_to_all x1 -> x2, waiting for transfers between devices: 93 us -> 39 us  [the longest x1 39 us: shards(): lax.all_to_all(pack_kv(send_index, kv, documents, length), 'dp', split_ax...]
    unnamed x28 -> x10, local copies, waits for them, and re-layouts: 35.7 us -> 1.21 us
    gather x16 -> x0, local copies, waits for them, and re-layouts: 34.3 us -> none  [the longest x8 23.6 us: unpack_rows(): return jnp.take(flat, keep_index, axis=0)]
    pallas_call x0 -> x3, Pallas kernels: none -> 19.4 us  [the longest x1 9.61 us: attend(): pl.pallas_call(functools.partial(attend_kernel, group_width // HEAD_SIZE)...]
    all_gather x1, waiting for transfers between devices: 103 us -> 92.6 us  [project(): lax.all_gather(key_value_weight, 'fsdp', axis=1, tiled=True)]
    mul x1 -> x0, other arithmetic: 6.83 us -> none  [pack_rows(): sent = taken * send_valid.astype(flat_rows.dtype)]
    dot_general x2 -> x0, matrix products: 6.19 us -> none  [the longest x1 3.12 us: attend(): jnp.einsum('mhgqk,mkhd->mqhgd', weights.astype(jnp.float32), key_value_he...]
    reduce_scatter x1, waiting for transfers between devices: 27.2 us -> 32 us  [project(): lax.psum_scatter(partial_value, 'tensor', scatter_dimension=1, tiled=True)]
  transfers between devices with their start and end apart: 3 -> 4, of which waited for: 3 -> 3; matrix products, arithmetic and copies ran while one was open for 2% -> 5% of each run, Pallas kernels for 0% -> 4%
where the time goes in v1:
time: 226 us; the launch traced here: 225 us
  waiting for transfers between devices  164 us (73%)
  Pallas kernels  19.4 us (9%)
  between operations  13.4 us (6%)
  matrix products  9.54 us (4%)
  starting transfers between devices  9.21 us (4%)
  blocking collectives  5.61 us (2%)
    all_gather x1, waiting for transfers between devices, project(): lax.all_gather(key_value_weight, 'fsdp', axis=1, tiled=True)  92.6 us
    all_to_all x1, waiting for transfers between devices, shards(): lax.all_to_all(pack_kv(send_index, kv, documents, length), 'dp', split_ax...  39 us
    reduce_scatter x1, waiting for transfers between devices, project(): lax.psum_scatter(partial_value, 'tensor', scatter_dimension=1, tiled=True)  32 us
    pallas_call x1, Pallas kernels, attend(): pl.pallas_call(functools.partial(attend_kernel, group_width // HEAD_SIZE)...  9.61 us
    dot_general x1, matrix products, project(): jnp.dot(normed, lax.all_gather(key_value_weight, 'fsdp', axis=1, tiled=Tr...  9.54 us
    psum x1, blocking collectives, project(): stats = lax.psum(jnp.sum(values * values, axis=1), 'tensor')  5.61 us
    all_to_all x1, starting transfers between devices, shards(): lax.all_to_all(pack_queries(send_index, queries, length), 'dp', split_axi...  5.5 us
    pallas_call x1, Pallas kernels, pack_queries(): pl.pallas_call(pack_query_kernel, grid_spec=pltpu.PrefetchScalarGridSpec(...  5.4 us
  transfers between devices with their start and end apart: 4, of which 3 were waited for; matrix products, arithmetic and copies ran while one was open for 5% of the time, Pallas kernels for 4%

profile of v1, /device:TPU:0, one launch (start us, length us, event | category | flops | bytes accessed | tf_op | source)
XLA Modules:
  0.0 225.5 jit_solution(9959949476917739447)
XLA Ops:
  6.5 0.0 copy-start.2
  6.5 0.0 all-gather.2.cloned.1.call-start
  6.5 0.7 all-gather.2.cloned.1.call-update
  7.3 0.0 copy-done.2
  7.3 0.1 and_select_fusion
  7.4 0.6 fusion.8.send_ref
  7.9 5.4 %pack_queries.1 = bf16[512,4096]{1,0:T(8,128)(2,1)} custom-call(s32[4]{0:T(128)} %fusion.8.send_ref, bf16[256,4096]{1,0:T(8,128)(2,1)} %query_ref.1), custom_call_target="tpu_custom_call" | custom-call | tf_op jit(solution)/shard_map/pack_queries/pallas_call | solution.py:23
  13.3 0.0 copy-start.1
  13.3 0.0 copy-start.3
  13.3 5.5 %all-to-all-start = ((bf16[4,128,4096]{2,1,0:T(8,128)(2,1)}), bf16[4,128,4096]{2,1,0:T(8,128)(2,1)}, u32[]{:S(2)}, u32[]{:S(2)}) async-start(bf16[4,128,4096]{2,1,0:T(8,128)(2,1)} %bitcast.11), calls=%async_computation | async-start | bytes 8388608 | tf_op jit(solution)/shard_map/all_to_all | solution.py:156
  18.9 0.0 reduce-scatter.2.cloned.1.call-start
  18.9 0.0 copy-done.1
  18.9 0.5 fusion
  19.3 5.6 %psum.7 = f32[256]{0:T(256)S(1)} all-reduce(f32[256]{0:T(256)S(1)} %fusion), channel_id=1, replica_groups=mesh['dp'=4,'fsdp'=4,'tensor'=2] {'tensor'}, use_global_device_ids=true, to_apply=%region_3.4 | all-reduce | flops 256 | bytes 2048 | tf_op jit(solution)/shard_map/psum | solution.py:129
  25.0 0.0 copy-start.4
  25.0 92.6 %all-gather.2.cloned.1.call-done = bf16[4096,2048]{1,0:T(8,128)(2,1)} async-done(((bf16[4096,512]{1,0:T(8,128)(2,1)}), bf16[4096,2048]{1,0:T(8,128)(2,1)}) %all-gather.2.cloned.1.call-update) | async-done | bytes 16777232 | tf_op jit(solution)/shard_map/all_gather | solution.py:135
  117.5 0.0 copy-done.3
  117.5 9.5 %fusion.3 = f32[256,2048]{1,0:T(8,128)} fusion(bf16[4096,2048]{1,0:T(8,128)(2,1)} %all-gather.2.cloned.1.call-done, bf16[256,4096]{1,0:T(8,128)(2,1)S(1)} %copy-done.1, f32[4096]{0:T(1024)S(1)} %copy-done.3, f32[256]{0:T(256)S(1)} %add_rsqrt_fusion), kind=kOutput, calls=%fused_computation.5 | convolution fusion | flops 4299161600 | bytes 20988928 | tf_op jit(solution)/shard_map/dot_general | solution.py:133
  127.1 0.0 reduce-scatter.2.cloned.1.call-update
  127.1 0.0 copy-done.4
  127.1 32.0 %reduce-scatter.2.cloned.1.call-done.kv_ref = f32[256,1024]{1,0:T(8,128)} async-done(((f32[256,2048]{1,0:T(8,128)}), f32[256,1024]{1,0:T(8,128)}) %reduce-scatter.2.cloned.1.call-update) | async-done | bytes 1048592 | tf_op jit(solution)/shard_map/reduce_scatter | solution.py:138
  159.2 0.7 broadcast_in_dim.41.document_ref
  159.9 4.4 %pack_kv.1 = bf16[512,1664]{1,0:T(8,128)(2,1)} custom-call(s32[4]{0:T(128)} %fusion.8.send_ref, f32[256,1024]{1,0:T(8,128)} %reduce-scatter.2.cloned.1.call-done.kv_ref, bf16[256,128]{1,0:T(8,128)(2,1)} %broadcast_in_dim.41.document_ref), custom_call_target="tpu_custom_call" | custom-call | tf_op jit(solution)/shard_map/pack_kv/pallas_call | solution.py:53
  164.4 0.0 all-to-all-done
  164.4 3.7 %all-to-all-start.1 = ((bf16[4,128,1664]{2,1,0:T(8,128)(2,1)}), bf16[4,128,1664]{2,1,0:T(8,128)(2,1)S(1)}, u32[]{:S(2)}, u32[]{:S(2)}) async-start(bf16[4,128,1664]{2,1,0:T(8,128)(2,1)} %bitcast.12), calls=%async_computation.2 | async-start | bytes 3407872 | tf_op jit(solution)/shard_map/all_to_all | solution.py:164
  168.1 0.8 fusion.7.keep_ref
  168.8 39.0 %all-to-all-done.1 = bf16[4,128,1664]{2,1,0:T(8,128)(2,1)S(1)} async-done(((bf16[4,128,1664]{2,1,0:T(8,128)(2,1)}), bf16[4,128,1664]{2,1,0:T(8,128)(2,1)S(1)}, u32[]{:S(2)}, u32[]{:S(2)}) %all-to-all-start.1) | async-done | bytes 1703968 | tf_op jit(solution)/shard_map/all_to_all | solution.py:164
  207.8 0.0 copy-start
  207.8 1.2 copy-done
  209.0 9.6 %attend.1 = bf16[256,4096]{1,0:T(8,128)(2,1)} custom-call(s32[2]{0:T(128)} %fusion.7.keep_ref, bf16[512,4096]{1,0:T(8,128)(2,1)} %bitcast.1.query_ref, bf16[512,1664]{1,0:T(8,128)(2,1)} %bitcast.7, bf16[512,1664]{1,0:T(8,128)(2,1)} %bitcast.8, bf16[512,1664]{1,0:T(8,128)(2,1)} %bitcast.9, bf16[512,1664]{1,0:T(8,128)(2,1)} %bitcast.10), custom_call_target="tpu_custom_call" | custom-call | tf_op jit(solution)/shard_map/attend/pallas_call | solution.py:108
  (4 shorter events, 0.0 us)
Async XLA Ops:
  6.5 0.7 copy-start.2
  6.5 111.0 %all-gather.2.cloned.1.call-start = ((), (), s32[]{:S(2)}) async-start(), calls=%async_computation.3 | async-start | bytes 20971520 | tf_op jit(solution)/shard_map/all_gather | solution.py:135
  13.3 5.5 %copy-start.1 = (bf16[256,4096]{1,0:T(8,128)(2,1)S(1)}, bf16[256,4096]{1,0:T(8,128)(2,1)}, u32[]{:S(2)}) copy-start(bf16[256,4096]{1,0:T(8,128)(2,1)} %param.6) | copy-start | bytes 6291460
  13.3 104.2 %copy-start.3 = (f32[4096]{0:T(1024)S(1)}, f32[4096]{0:T(1024)}, u32[]{:S(2)}) copy-start(f32[4096]{0:T(1024)} %param.9) | copy-start | bytes 49156
  13.3 151.0 %all-to-all-start = ((bf16[4,128,4096]{2,1,0:T(8,128)(2,1)}), bf16[4,128,4096]{2,1,0:T(8,128)(2,1)}, u32[]{:S(2)}, u32[]{:S(2)}) async-start(bf16[4,128,4096]{2,1,0:T(8,128)(2,1)} %bitcast.11), calls=%async_computation | async-start | bytes 8388608 | tf_op jit(solution)/shard_map/all_to_all | solution.py:156
  18.9 140.3 %reduce-scatter.2.cloned.1.call-start = ((), (), s32[]{:S(2)}) async-start(), calls=%async_computation.4 | async-start | bytes 3145728 | tf_op jit(solution)/shard_map/reduce_scatter | solution.py:138
  25.0 102.1 %copy-start.4 = (s32[2,128]{1,0:T(2,128)S(1)}, s32[2,128]{1,0:T(2,128)}, u32[]{:S(2)}) copy-start(s32[2,128]{1,0:T(2,128)} %param.8) | copy-start | bytes 3076
  164.4 43.5 %all-to-all-start.1 = ((bf16[4,128,1664]{2,1,0:T(8,128)(2,1)}), bf16[4,128,1664]{2,1,0:T(8,128)(2,1)S(1)}, u32[]{:S(2)}, u32[]{:S(2)}) async-start(bf16[4,128,1664]{2,1,0:T(8,128)(2,1)} %bitcast.12), calls=%async_computation.2 | async-start | bytes 3407872 | tf_op jit(solution)/shard_map/all_to_all | solution.py:164
  207.8 1.2 copy-start
Sparse Core Ops, SparseCore 0:
  8.9 108.6 all-gather.1
  127.2 31.8 reduce-scatter.1

commit v2 on v1

--- a/solution.py
+++ b/solution.py
@@ -7,6 +7,7 @@
 from jax.experimental.pallas import tpu as pltpu
 from jax.sharding import PartitionSpec as P
 
+
 HEAD_SIZE = 128
 
 
@@ -33,37 +34,76 @@
     )(send_index, queries)
 
 
-def pack_kv_kernel(heads_kv, send_ref, kv_ref, document_ref, out_ref):
+def split_partial_kernel(part_ref, out_ref):
+    key = part_ref[:, :HEAD_SIZE]
+    high = key.astype(jnp.bfloat16)
+    out_ref[:, :HEAD_SIZE] = high
+    out_ref[:, HEAD_SIZE : 2 * HEAD_SIZE] = (key - high.astype(jnp.float32)).astype(jnp.bfloat16)
+    out_ref[:, 2 * HEAD_SIZE :] = part_ref[:, HEAD_SIZE:].astype(jnp.bfloat16)
+
+
+def split_partial(partial_value, ranks, spread):
+    rows, width = partial_value.shape
+    all_heads = width // (2 * HEAD_SIZE)
+    heads = all_heads // spread
+    height = rows // ranks
+    return pl.pallas_call(
+        split_partial_kernel,
+        grid=(spread, ranks, heads),
+        in_specs=[pl.BlockSpec((height, 2 * HEAD_SIZE), lambda b, f, h: (f, b * heads + h))],
+        out_specs=pl.BlockSpec(
+            (height, 3 * HEAD_SIZE), lambda b, f, h: ((b * ranks + f) * heads + h, 0)
+        ),
+        out_shape=jax.ShapeDtypeStruct((ranks * all_heads * height, 3 * HEAD_SIZE), jnp.bfloat16),
+        name="split_partial",
+    )(partial_value)
+
+
+def pack_kv_kernel(sources, send_ref, slot_ref, *refs):
+    *part_refs, document_ref, out_ref = refs
+    part_heads = part_refs[0].shape[1]
+    heads_kv = part_heads * len(part_refs) // sources
     for h in range(heads_kv):
-        key = kv_ref[:, 2 * h * HEAD_SIZE : (2 * h + 1) * HEAD_SIZE]
+        first = h // part_heads * sources
+        key = value = 0.0
+        for part_ref in part_refs[first : first + sources]:
+            block = part_ref[0, h % part_heads, 0].astype(jnp.float32)
+            key += block[:, :HEAD_SIZE] + block[:, HEAD_SIZE : 2 * HEAD_SIZE]
+            value += block[:, 2 * HEAD_SIZE :]
         high = key.astype(jnp.bfloat16)
         low = (key - high.astype(jnp.float32)).astype(jnp.bfloat16)
-        value = kv_ref[:, (2 * h + 1) * HEAD_SIZE : (2 * h + 2) * HEAD_SIZE]
         for place, part in enumerate((high, low, value.astype(jnp.bfloat16))):
             start = (place * heads_kv + h) * HEAD_SIZE
             out_ref[:, start : start + HEAD_SIZE] = part
     out_ref[:, 3 * heads_kv * HEAD_SIZE :] = document_ref[...]
 
 
-def pack_kv(send_index, kv, documents, length):
+def pack_kv(send_index, slot_index, parts, documents, sources, length):
     ranks = send_index.shape[0]
-    width = kv.shape[1]
-    heads_kv = width // (2 * HEAD_SIZE)
-    packed = (3 * heads_kv + 1) * HEAD_SIZE
-    return pl.pallas_call(
-        functools.partial(pack_kv_kernel, heads_kv),
+    count = slot_index.shape[0]
+    rows = documents.shape[0]
+    part_heads = parts.shape[0] // (count * rows)
+    packed = (3 * part_heads * count // sources + 1) * HEAD_SIZE
+
+    def arrived(w):
+        return pl.BlockSpec(
+            (1, part_heads, 1, length, 3 * HEAD_SIZE),
+            lambda r, send, slot: (slot[w], 0, send[r], 0, 0),
+        )
+
+    view = parts.reshape(count, part_heads, rows // length, length, 3 * HEAD_SIZE)
+    return pl.pallas_call(
+        functools.partial(pack_kv_kernel, sources),
         grid_spec=pltpu.PrefetchScalarGridSpec(
-            num_scalar_prefetch=1,
+            num_scalar_prefetch=2,
             grid=(ranks,),
-            in_specs=[
-                pl.BlockSpec((length, width), lambda r, send: (send[r], 0)),
-                pl.BlockSpec((length, HEAD_SIZE), lambda r, send: (send[r], 0)),
-            ],
-            out_specs=pl.BlockSpec((length, packed), lambda r, send: (r, 0)),
+            in_specs=[arrived(w) for w in range(count)]
+            + [pl.BlockSpec((length, HEAD_SIZE), lambda r, send, slot: (send[r], 0))],
+            out_specs=pl.BlockSpec((length, packed), lambda r, send, slot: (r, 0)),
         ),
         out_shape=jax.ShapeDtypeStruct((ranks * length, packed), jnp.bfloat16),
         name="pack_kv",
-    )(send_index, kv, documents)
+    )(send_index, slot_index, *[view] * count, documents)
 
 
 def attend_kernel(
@@ -125,17 +165,33 @@
 
 
 def project(rows, gain, key_value_weight):
+    all_rows = lax.all_gather(rows, "fsdp", axis=0, tiled=True)
     values = rows.astype(jnp.float32)
-    stats = lax.psum(jnp.sum(values * values, axis=1), "tensor")
+    own_stats = jnp.sum(values * values, axis=1)
+    stats = lax.psum(own_stats, "tensor")
     full_width = rows.shape[1] * lax.axis_size("tensor")
-    scale = lax.rsqrt(stats / full_width + epsilon)
-    normed = (values * scale[:, None] * gain).astype(jnp.bfloat16)
-    partial_value = jnp.dot(
-        normed,
-        lax.all_gather(key_value_weight, "fsdp", axis=1, tiled=True),
-        preferred_element_type=jnp.float32,
-    )
-    return lax.psum_scatter(partial_value, "tensor", scatter_dimension=1, tiled=True)
+    scale = lax.all_gather(lax.rsqrt(stats / full_width + epsilon), "fsdp", axis=0, tiled=True)
+    normed = (all_rows.astype(jnp.float32) * scale[:, None] * gain).astype(jnp.bfloat16)
+    partial_value = jnp.dot(normed, key_value_weight, preferred_element_type=jnp.float32)
+    f_ranks, t_ranks = lax.axis_size("fsdp"), lax.axis_size("tensor")
+    joined, spread = max(1, f_ranks // t_ranks), max(1, t_ranks // f_ranks)
+    count = f_ranks * spread
+    parts = split_partial(partial_value, f_ranks, spread)
+    share = parts.shape[0] // count
+    f, t = lax.axis_index("fsdp"), lax.axis_index("tensor")
+    number = f % joined * t_ranks + t
+    arrived = []
+    for p in range(count):
+        pairs = []
+        for i in range(f_ranks):
+            for j in range(t_ranks):
+                block = (i % joined * t_ranks + j + p) % count
+                target = i // joined * spread + block // f_ranks
+                pairs.append((i * t_ranks + j, block % f_ranks * t_ranks + target))
+        sent = lax.dynamic_slice_in_dim(parts, (number + p) % count * share, share)
+        arrived.append(lax.ppermute(sent, ("fsdp", "tensor"), pairs))
+    slot_index = (t % spread * f_ranks + f - jnp.arange(count, dtype=jnp.int32)) % count
+    return jnp.concatenate(arrived), slot_index
 
 
 def shards(tokens, queries, segment_ids, gain, key_value_weight, plan):
@@ -153,17 +209,18 @@
     keep_index = jnp.sum(
         jnp.where(plan[None, :] == own_slots[:, None], position[None, :] // batches, 0), axis=1
     )
-    moved_queries = lax.all_to_all(
-        pack_queries(send_index, queries, length), "dp", split_axis=0, concat_axis=0, tiled=True
-    )
+    parcels = pack_queries(send_index, queries, length)
+    moved_queries = lax.all_to_all(parcels, "dp", split_axis=0, concat_axis=0, tiled=True)
     documents = jnp.broadcast_to(
         segment_ids.reshape(batches * length, 1).astype(jnp.bfloat16),
         (batches * length, HEAD_SIZE),
     )
-    kv = project(tokens, gain, key_value_weight)
-    moved_kv = lax.all_to_all(
-        pack_kv(send_index, kv, documents, length), "dp", split_axis=0, concat_axis=0, tiled=True
-    )
+    parts, slot_index = project(tokens, gain, key_value_weight)
+    packed = pack_kv(
+        send_index, slot_index, parts, documents, lax.axis_size("tensor"), length
+    )
+    packed, moved_queries = lax.optimization_barrier((packed, moved_queries))
+    moved_kv = lax.all_to_all(packed, "dp", split_axis=0, concat_axis=0, tiled=True)
     return attend(keep_index, moved_queries, moved_kv, length)
 
 

time: 226 us -> 180 us (0.80)
  waiting for transfers between devices: 164 us -> 93.1 us
  starting transfers between devices: 9.21 us -> 17.5 us
  Pallas kernels: 19.4 us -> 25.9 us
  blocking collectives: 5.61 us -> 10.1 us
  other arithmetic: 1.94 us -> 4.6 us
    all_gather x1, waiting for transfers between devices: 92.6 us -> 38.7 us  [project(): all_rows = lax.all_gather(rows, 'fsdp', axis=0, tiled=True)]
    reduce_scatter x1 -> x0, waiting for transfers between devices: 32 us -> none  [project(): lax.psum_scatter(partial_value, 'tensor', scatter_dimension=1, tiled=True)]
    ppermute x0 -> x4, waiting for transfers between devices: none -> 13.9 us  [project(): arrived.append(lax.ppermute(sent, ('fsdp', 'tensor'), pairs))]
    ppermute x0 -> x4, starting transfers between devices: none -> 6.45 us  [project(): arrived.append(lax.ppermute(sent, ('fsdp', 'tensor'), pairs))]
    pallas_call x1 -> x2, Pallas kernels: 4.44 us -> 10.7 us  [the longest x1 5.57 us: split_partial(): pl.pallas_call(split_partial_kernel, grid=(spread, ranks, heads), in_spec...]
    all_gather x0 -> x1, blocking collectives: none -> 5.2 us  [project(): lax.all_gather(lax.rsqrt(stats / full_width + epsilon), 'fsdp', axis=0, t...]
  transfers between devices with their start and end apart: 4 -> 7, of which waited for: 3 -> 5; matrix products, arithmetic and copies ran while one was open for 5% -> 10% of each run, Pallas kernels for 4% -> 9%
where the time goes in v2:
time: 180 us; the launch traced here: 179 us
  waiting for transfers between devices  93.1 us (52%)
  Pallas kernels  25.9 us (14%)
  starting transfers between devices  17.5 us (10%)
  between operations  13.5 us (8%)
  matrix products  10.4 us (6%)
  blocking collectives  10.1 us (6%)
  other arithmetic  4.6 us (3%)
  local copies, waits for them, and re-layouts  3.45 us (2%)
    all_to_all x1, waiting for transfers between devices, shards(): lax.all_to_all(packed, 'dp', split_axis=0, concat_axis=0, tiled=True)  39.8 us
    all_gather x1, waiting for transfers between devices, project(): all_rows = lax.all_gather(rows, 'fsdp', axis=0, tiled=True)  38.7 us
    ppermute x4, waiting for transfers between devices, project(): arrived.append(lax.ppermute(sent, ('fsdp', 'tensor'), pairs))  13.9 us
    dot_general x1, matrix products, project(): jnp.dot(normed, key_value_weight, preferred_element_type=jnp.float32)  10.4 us
    pallas_call x1, Pallas kernels, attend(): pl.pallas_call(functools.partial(attend_kernel, group_width // HEAD_SIZE)...  9.61 us
    ppermute x4, starting transfers between devices, project(): arrived.append(lax.ppermute(sent, ('fsdp', 'tensor'), pairs))  6.45 us
    all_to_all x1, starting transfers between devices, shards(): lax.all_to_all(parcels, 'dp', split_axis=0, concat_axis=0, tiled=True)  6.23 us
    pallas_call x1, Pallas kernels, pack_queries(): pl.pallas_call(pack_query_kernel, grid_spec=pltpu.PrefetchScalarGridSpec(...  5.65 us
  transfers between devices with their start and end apart: 7, of which 5 were waited for; matrix products, arithmetic and copies ran while one was open for 10% of the time, Pallas kernels for 9%

profile of v2, /device:TPU:0, one launch (start us, length us, event | category | flops | bytes accessed | tf_op | source)
XLA Modules:
  0.0 178.7 jit_solution(13486197908661210889)
XLA Ops:
  6.5 0.0 all-gather.3.cloned.1.call-start
  6.5 0.7 all-gather.3.cloned.1.call-update
  7.3 0.7 and_select_fusion.1
  8.0 0.7 fusion.4.send_ref
  8.7 5.7 %pack_queries.1 = bf16[512,4096]{1,0:T(8,128)(2,1)} custom-call(s32[4]{0:T(128)} %fusion.4.send_ref, bf16[256,4096]{1,0:T(8,128)(2,1)} %query_ref.1), custom_call_target="tpu_custom_call" | custom-call | tf_op jit(solution)/shard_map/pack_queries/pallas_call | solution.py:24
  14.3 0.0 copy-start.1
  14.3 0.0 copy-start.3
  14.3 6.2 %all-to-all-start = ((bf16[4,128,4096]{2,1,0:T(8,128)(2,1)}), bf16[4,128,4096]{2,1,0:T(8,128)(2,1)}, u32[]{:S(2)}, u32[]{:S(2)}) async-start(bf16[4,128,4096]{2,1,0:T(8,128)(2,1)} %bitcast.18), calls=%async_computation | async-start | bytes 8388608 | tf_op jit(solution)/shard_map/all_to_all | solution.py:213
  20.6 0.0 copy-done.1
  20.6 0.5 multiply_reduce_fusion
  21.1 4.9 %psum.7 = f32[256]{0:T(256)S(1)} all-reduce(f32[256]{0:T(256)S(1)} %multiply_reduce_fusion), channel_id=1, replica_groups=mesh['dp'=4,'fsdp'=4,'tensor'=2] {'tensor'}, use_global_device_ids=true, to_apply=%region_3.4 | all-reduce | flops 256 | bytes 2048 | tf_op jit(solution)/shard_map/psum | solution.py:171
  26.0 5.2 %all-gather = f32[4,1,256]{2,1,0:T(1,128)S(1)} all-gather(f32[1,1,256]{2,1,0:T(1,128)S(1)} %bitcast.21), channel_id=1, replica_groups=mesh['dp'=4,'fsdp'=4,'tensor'=2] {'fsdp'}, dimensions={0}, use_global_device_ids=true | all-gather | bytes 5120 | tf_op jit(solution)/shard_map/all_gather | solution.py:173
  31.2 38.7 %all-gather.3.cloned.1.call-done = bf16[1024,4096]{1,0:T(8,128)(2,1)} async-done(((bf16[256,4096]{1,0:T(8,128)(2,1)}), bf16[1024,4096]{1,0:T(8,128)(2,1)}) %all-gather.3.cloned.1.call-update) | async-done | bytes 8388624 | tf_op jit(solution)/shard_map/all_gather | solution.py:168
  69.9 0.0 copy-done.3
  69.9 10.4 %fusion.part_ref = f32[1024,512]{1,0:T(8,128)} fusion(bf16[4096,512]{1,0:T(8,128)(2,1)} %param.10, bf16[1024,4096]{1,0:T(8,128)(2,1)} %all-gather.3.cloned.1.call-done, f32[4096]{0:T(1024)S(1)} %copy-done.3, f32[1024]{0:T(1024)S(1)} %bitcast.20), kind=kOutput, calls=%fused_computation.1 | convolution fusion | flops 4311744512 | bytes 14700544 | tf_op jit(solution)/shard_map/dot_general | solution.py:175
  80.4 0.0 copy-start.4
  80.4 5.6 %split_partial.1 = bf16[2048,384]{1,0:T(8,128)(2,1)} custom-call(f32[1024,512]{1,0:T(8,128)} %fusion.part_ref), custom_call_target="tpu_custom_call" | custom-call | tf_op jit(solution)/shard_map/split_partial/pallas_call | solution.py:50
  85.9 1.5 constant_dynamic-slice_fusion.3
  87.4 2.1 %collective-permute-start.3 = (bf16[512,384]{1,0:T(8,128)(2,1)S(1)}, bf16[512,384]{1,0:T(8,128)(2,1)S(1)}, u32[]{:S(2)}, u32[]{:S(2)}) collective-permute-start(bf16[512,384]{1,0:T(8,128)(2,1)S(1)} %get-tuple-element.10), channel_id=1, source_target_pairs={{0,6},{1,0},{2,2},{3,4},{4,7},{5,1},{6,3},{7,5},{8,14},{9,8},{10,1... | collective-permute-start | bytes 1179656 | tf_op jit(solution)/shard_map/ppermute | solution.py:192
  89.6 1.7 collective-permute-start.2
  91.3 1.9 %collective-permute-start.1 = (bf16[512,384]{1,0:T(8,128)(2,1)S(1)}, bf16[512,384]{1,0:T(8,128)(2,1)S(1)}, u32[]{:S(2)}, u32[]{:S(2)}) collective-permute-start(bf16[512,384]{1,0:T(8,128)(2,1)S(1)} %get-tuple-element.12), channel_id=1, source_target_pairs={{0,2},{1,4},{2,6},{3,0},{4,3},{5,5},{6,7},{7,1},{8,10},{9,12},{10,... | collective-permute-start | bytes 1179656 | tf_op jit(solution)/shard_map/ppermute | solution.py:192
  93.2 0.7 collective-permute-start
  93.9 0.6 and_select_fusion.slot_ref
  94.5 0.0 copy-done.4
  94.5 6.8 %collective-permute-done.3 = bf16[512,384]{1,0:T(8,128)(2,1)S(1)} collective-permute-done((bf16[512,384]{1,0:T(8,128)(2,1)S(1)}, bf16[512,384]{1,0:T(8,128)(2,1)S(1)}, u32[]{:S(2)}, u32[]{:S(2)}) %collective-permute-start.3) | collective-permute-done | bytes 393248 | tf_op jit(solution)/shard_map/ppermute | solution.py:192
  101.3 1.8 collective-permute-done.2
  103.1 5.3 %collective-permute-done.1 = bf16[512,384]{1,0:T(8,128)(2,1)S(1)} collective-permute-done((bf16[512,384]{1,0:T(8,128)(2,1)S(1)}, bf16[512,384]{1,0:T(8,128)(2,1)S(1)}, u32[]{:S(2)}, u32[]{:S(2)}) %collective-permute-start.1) | collective-permute-done | bytes 393248 | tf_op jit(solution)/shard_map/ppermute | solution.py:192
  108.4 0.0 collective-permute-done
  108.4 1.3 pad_maximum_fusion
  109.7 0.7 broadcast_in_dim.41.refs_4_
  110.4 5.1 %pack_kv.1 = bf16[512,1664]{1,0:T(8,128)(2,1)} custom-call(s32[4]{0:T(128)} %fusion.4.send_ref, s32[4]{0:T(128)} %and_select_fusion.slot_ref, bf16[4,2,2,128,384]{4,3,2,1,0:T(8,128)(2,1)} %bitcast.14, bf16[4,2,2,128,384]{4,3,2,1,0:T(8,128)(2,1)} %bitcast.15, bf16[4,2,2,128,384]{4,3,2,1,0:T(8,128)(2,1)} %bitcast.16, bf16[4,2,2,128,384]{4,3,2,1,0:T(8,128)(2,1)} %bitcast.17, ...), custom_call_target="tpu_custom_call" | custom-call | tf_op jit(solution)/shard_map/pack_kv/pallas_call | solution.py:95
  115.5 0.0 copy-start.2
  115.5 0.0 all-to-all-done
  115.5 4.9 %all-to-all-start.1 = ((bf16[4,128,1664]{2,1,0:T(8,128)(2,1)}), bf16[4,128,1664]{2,1,0:T(8,128)(2,1)S(1)}, u32[]{:S(2)}, u32[]{:S(2)}) async-start(bf16[4,128,1664]{2,1,0:T(8,128)(2,1)} %bitcast.19), calls=%async_computation.1 | async-start | bytes 3407872 | tf_op jit(solution)/shard_map/all_to_all | solution.py:223
  120.4 0.0 copy-done.2
  120.4 0.8 fusion.3.keep_ref
  121.2 39.8 %all-to-all-done.1 = bf16[4,128,1664]{2,1,0:T(8,128)(2,1)S(1)} async-done(((bf16[4,128,1664]{2,1,0:T(8,128)(2,1)}), bf16[4,128,1664]{2,1,0:T(8,128)(2,1)S(1)}, u32[]{:S(2)}, u32[]{:S(2)}) %all-to-all-start.1) | async-done | bytes 1703968 | tf_op jit(solution)/shard_map/all_to_all | solution.py:223
  161.0 0.0 copy-start
  161.0 1.2 copy-done
  162.2 9.6 %attend.1 = bf16[256,4096]{1,0:T(8,128)(2,1)} custom-call(s32[2]{0:T(128)} %fusion.3.keep_ref, bf16[512,4096]{1,0:T(8,128)(2,1)} %bitcast.5.query_ref, bf16[512,1664]{1,0:T(8,128)(2,1)} %bitcast.10, bf16[512,1664]{1,0:T(8,128)(2,1)} %bitcast.11, bf16[512,1664]{1,0:T(8,128)(2,1)} %bitcast.12, bf16[512,1664]{1,0:T(8,128)(2,1)} %bitcast.13), custom_call_target="tpu_custom_call" | custom-call | tf_op jit(solution)/shard_map/attend/pallas_call | solution.py:148
  (4 shorter events, 0.0 us)
Async XLA Ops:
  6.5 63.4 %all-gather.3.cloned.1.call-start = ((), (), s32[]{:S(2)}) async-start(), calls=%async_computation.2 | async-start | bytes 10485760 | tf_op jit(solution)/shard_map/all_gather | solution.py:168
  14.3 6.2 %copy-start.1 = (bf16[256,4096]{1,0:T(8,128)(2,1)S(1)}, bf16[256,4096]{1,0:T(8,128)(2,1)}, u32[]{:S(2)}) copy-start(bf16[256,4096]{1,0:T(8,128)(2,1)} %param.6) | copy-start | bytes 6291460
  14.3 55.6 %copy-start.3 = (f32[4096]{0:T(1024)S(1)}, f32[4096]{0:T(1024)}, u32[]{:S(2)}) copy-start(f32[4096]{0:T(1024)} %param.9) | copy-start | bytes 49156
  14.3 101.2 %all-to-all-start = ((bf16[4,128,4096]{2,1,0:T(8,128)(2,1)}), bf16[4,128,4096]{2,1,0:T(8,128)(2,1)}, u32[]{:S(2)}, u32[]{:S(2)}) async-start(bf16[4,128,4096]{2,1,0:T(8,128)(2,1)} %bitcast.18), calls=%async_computation | async-start | bytes 8388608 | tf_op jit(solution)/shard_map/all_to_all | solution.py:213
  80.4 14.1 %copy-start.4 = (s32[2,128]{1,0:T(2,128)S(1)}, s32[2,128]{1,0:T(2,128)}, u32[]{:S(2)}) copy-start(s32[2,128]{1,0:T(2,128)} %param.8) | copy-start | bytes 3076
  87.4 13.9 %collective-permute-start.3 = (bf16[512,384]{1,0:T(8,128)(2,1)S(1)}, bf16[512,384]{1,0:T(8,128)(2,1)S(1)}, u32[]{:S(2)}, u32[]{:S(2)}) collective-permute-start(bf16[512,384]{1,0:T(8,128)(2,1)S(1)} %get-tuple-element.10), channel_id=1, source_target_pairs={{0,6},{1,0},{2,2},{3,4},{4,7},{5,1},{6,3},{7,5},{8,14},{9,8},{10,1... | collective-permute-start | bytes 1179656 | tf_op jit(solution)/shard_map/ppermute | solution.py:192
  89.6 13.5 %collective-permute-start.2 = (bf16[512,384]{1,0:T(8,128)(2,1)S(1)}, bf16[512,384]{1,0:T(8,128)(2,1)S(1)}, u32[]{:S(2)}, u32[]{:S(2)}) collective-permute-start(bf16[512,384]{1,0:T(8,128)(2,1)S(1)} %get-tuple-element.11), channel_id=1, source_target_pairs={{0,4},{1,6},{2,0},{3,2},{4,5},{5,7},{6,1},{7,3},{8,12},{9,14},{10,... | collective-permute-start | bytes 1179656 | tf_op jit(solution)/shard_map/ppermute | solution.py:192
  91.3 17.1 %collective-permute-start.1 = (bf16[512,384]{1,0:T(8,128)(2,1)S(1)}, bf16[512,384]{1,0:T(8,128)(2,1)S(1)}, u32[]{:S(2)}, u32[]{:S(2)}) collective-permute-start(bf16[512,384]{1,0:T(8,128)(2,1)S(1)} %get-tuple-element.12), channel_id=1, source_target_pairs={{0,2},{1,4},{2,6},{3,0},{4,3},{5,5},{6,7},{7,1},{8,10},{9,12},{10,... | collective-permute-start | bytes 1179656 | tf_op jit(solution)/shard_map/ppermute | solution.py:192
  93.2 15.1 %collective-permute-start = (bf16[512,384]{1,0:T(8,128)(2,1)S(1)}, bf16[512,384]{1,0:T(8,128)(2,1)S(1)}, u32[]{:S(2)}, u32[]{:S(2)}) collective-permute-start(bf16[512,384]{1,0:T(8,128)(2,1)S(1)} %get-tuple-element.9), channel_id=1, source_target_pairs={{0,0},{1,2},{2,4},{3,6},{4,1},{5,3},{6,5},{7,7},{8,8},{9,10},{10,1... | collective-permute-start | bytes 1179656 | tf_op jit(solution)/shard_map/ppermute | solution.py:192
  115.5 4.9 %copy-start.2 = (s32[8]{0:T(128)S(1)}, s32[8]{0:T(128)}, u32[]{:S(2)}) copy-start(s32[8]{0:T(128)} %param.11) | copy-start | bytes 100
  115.5 45.5 %all-to-all-start.1 = ((bf16[4,128,1664]{2,1,0:T(8,128)(2,1)}), bf16[4,128,1664]{2,1,0:T(8,128)(2,1)S(1)}, u32[]{:S(2)}, u32[]{:S(2)}) async-start(bf16[4,128,1664]{2,1,0:T(8,128)(2,1)} %bitcast.19), calls=%async_computation.1 | async-start | bytes 3407872 | tf_op jit(solution)/shard_map/all_to_all | solution.py:223
  161.0 1.2 copy-start
Sparse Core Ops, SparseCore 0:
  8.9 60.9 all-gather.2
